TPU v7x, 32 devices: a whole 2x2x4 slice. The times are simulated.
32 devices in a mesh: row: 4 (over x, core), col: 8 (over z, y).
Axes of the slice: x: 2, y: 2, z: 4, core: 2. Of those that a mesh axis runs over, the one named last changes fastest.
Arguments:
- rhs_c: float32 [12, 512, 6, 1024], P(None, 'row', None, 'col'), may hold values from -6 to 6
- rhs_f: float32 [12, 512, 6, 1024], P(None, 'row', None, 'col'), may hold values from -6 to 6
- pencil_a: bfloat16 [12, 512, 6, 1024], P(None, 'row', None, 'col'), may hold values from -0.5 to 0.5
- pencil_d: bfloat16 [12, 512, 6, 1024], P(None, 'row', None, 'col'), may hold values from -0.5 to 0.5
- pencil_b: bfloat16 [12, 512, 6, 1024], P(None, 'row', None, 'col'), may hold values from -0.5 to 0.5
- pencil_e: bfloat16 [12, 512, 6, 1024], P(None, 'row', None, 'col'), may hold values from -0.5 to 0.5
- d_inverse: float32 [12, 512, 128], P(None, 'row'), may hold values from -0.25 to 2.5
- left_vectors: float32 [12, 512, 128], P(None, 'row'), may hold values from -0.25 to 2.5
- left_inverse: float32 [12, 512, 128], P(None, 'row'), may hold values from -0.25 to 2.5
- left_eigs: float32 [12, 512], P(None, 'row'), may hold values from 1 to 3
- e_inverse: float32 [6, 1024, 128], P(None, 'col'), may hold values from -0.25 to 2.5
- right_vectors: float32 [6, 1024, 128], P(None, 'col'), may hold values from -0.25 to 2.5
- right_inverse: float32 [6, 1024, 128], P(None, 'col'), may hold values from -0.25 to 2.5
- right_eigs: float32 [6, 1024], P(None, 'col'), may hold values from -3 to -1
Outputs:
- updated_c: float32 [12, 512, 6, 1024], P(None, 'row', None, 'col')
- updated_f: float32 [12, 512, 6, 1024], P(None, 'row', None, 'col')
- solved_r: float32 [12, 512, 6, 1024], P(None, 'row', None, 'col')
- solved_l: float32 [12, 512, 6, 1024], P(None, 'row', None, 'col')
All inputs are finite; a program needn't handle non-finite values.
Results may differ from a plain program's by a relative error of at most 0.0003.
Values may be sent and summed in bfloat16 or wider, within the bound.
A program may use at most 128 MiB of HBM per device.

v0:
```python
import jax
import jax.numpy as jnp
from jax import lax
from jax.sharding import PartitionSpec as P

TILE = 128
ORDER = 6144
STEPS = 3


def padded(value, sides, width):
    for axis, dim in sides:
        devices, length = (lax.axis_size(axis), value.shape[dim])
        up = [(i, (i + 1) % devices) for i in range(devices)]
        down = [(j, i) for i, j in up]
        last = lax.slice_in_dim(value, length - width, length, axis=dim)
        initial = lax.slice_in_dim(value, 0, width, axis=dim)
        before = lax.ppermute(last, axis, up)
        after = lax.ppermute(initial, axis, down)
        value = jnp.concatenate([before, value, after], axis=dim)
    return value


def product(left, right):
    return jnp.einsum("bij,bjk->bik", left, right, precision=lax.Precision.HIGHEST)


def solve_tiles(
    a_diag,
    e_diag,
    resid_c,
    resid_f,
    inv_d,
    vec_left,
    back_left,
    eig_left,
    inv_e,
    vec_right,
    back_right,
    eig_right,
):
    coupled = product(a_diag, inv_d)
    merged = product(resid_c - product(coupled, resid_f), inv_e)
    spectral = product(product(back_left, merged), vec_right)
    spectral = spectral / (eig_left[:, :, None] - eig_right[:, None, :])
    new_l = product(product(vec_left, spectral), back_right)
    new_r = product(inv_d, resid_f + product(new_l, e_diag))
    return (new_r, new_l)


def body(
    rhs_c,
    rhs_f,
    pencil_a,
    pencil_d,
    pencil_b,
    pencil_e,
    d_inverse,
    left_vectors,
    left_inverse,
    left_eigs,
    e_inverse,
    right_vectors,
    right_inverse,
    right_eigs,
):
    highest = lax.Precision.HIGHEST
    count_rows = lax.axis_size("row")
    count_cols = lax.axis_size("col")
    this_row = lax.axis_index("row")
    this_col = lax.axis_index("col")
    rows_dev = rhs_c.shape[0]
    cols_dev = rhs_c.shape[2]
    blocks = ORDER // TILE
    local_rows = jnp.arange(rows_dev, dtype=jnp.int32)
    local_cols = jnp.arange(cols_dev, dtype=jnp.int32)
    block_rows = local_rows * count_rows + this_row
    block_cols = local_cols * count_cols + this_col
    near_ad = padded(jnp.stack([pencil_a, pencil_d]), (("col", 4),), TILE)
    near_ad = near_ad.reshape(2, rows_dev, TILE, cols_dev, 3, TILE)
    near_be = padded(jnp.stack([pencil_b, pencil_e]), (("row", 2),), TILE)
    near_be = near_be.reshape(2, rows_dev, 3, TILE, cols_dev, TILE)
    current_c = rhs_c
    current_f = rhs_f
    out_r = jnp.zeros_like(rhs_c)
    out_l = jnp.zeros_like(rhs_c)
    for step in range(STEPS):
        offset = 1 - step
        front_rows = block_cols + offset
        col_valid = (front_rows >= 0) & (front_rows < blocks)
        rows_clip = jnp.clip(front_rows, 0, blocks - 1)
        front_cols = block_rows - offset
        row_valid = (front_cols >= 0) & (front_cols < blocks)
        cols_clip = jnp.clip(front_cols, 0, blocks - 1)
        slot_cols = jnp.clip(rows_clip // count_cols, 0, cols_dev - 1)
        picked_ad = jnp.take(near_ad[:, :, :, :, 1 + offset, :], slot_cols, axis=3)
        panel_a = picked_ad[0]
        panel_d = picked_ad[1]
        slot_rows = jnp.clip(cols_clip // count_rows, 0, rows_dev - 1)
        picked_be = jnp.take(near_be[:, :, 1 - offset, :, :, :], slot_rows, axis=1)
        panel_b = picked_be[0]
        panel_e = picked_be[1]
        owned = col_valid & (rows_clip % count_rows == this_row)
        own_slot = jnp.clip(rows_clip // count_rows, 0, rows_dev - 1)
        resid_c = current_c[own_slot, :, local_cols, :]
        resid_f = current_f[own_slot, :, local_cols, :]
        a_diag = panel_a[own_slot, :, local_cols, :].astype(jnp.float32)
        e_diag = panel_e[own_slot, :, local_cols, :].astype(jnp.float32)
        new_r, new_l = solve_tiles(
            a_diag,
            e_diag,
            resid_c,
            resid_f,
            d_inverse[own_slot],
            left_vectors[own_slot],
            left_inverse[own_slot],
            left_eigs[own_slot],
            e_inverse,
            right_vectors,
            right_inverse,
            right_eigs,
        )
        new_r = jnp.where(owned[:, None, None], new_r, 0.0)
        new_l = jnp.where(owned[:, None, None], new_l, 0.0)
        l_slot = jnp.clip(cols_clip // count_cols, 0, cols_dev - 1)
        front_r = lax.psum(new_r, "row")
        picked = jnp.where((cols_clip % count_cols == this_col)[:, None, None], new_l[l_slot], 0.0)
        front_l = lax.psum(picked, "col")
        front_r = jnp.where(col_valid[:, None, None], front_r, 0.0)
        front_l = jnp.where(row_valid[:, None, None], front_l, 0.0)
        mask_a = (block_rows[:, None] < front_rows[None, :]) & col_valid[None, :]
        term_c = jnp.einsum(
            "apbq,bqs->apbs", panel_a.astype(jnp.float32), front_r, precision=highest
        )
        term_f = jnp.einsum(
            "apbq,bqs->apbs", panel_d.astype(jnp.float32), front_r, precision=highest
        )
        mask_b = (block_cols[None, :] > front_cols[:, None]) & row_valid[:, None]
        gain_c = jnp.einsum(
            "apq,aqbs->apbs", front_l, panel_b.astype(jnp.float32), precision=highest
        )
        gain_f = jnp.einsum(
            "apq,aqbs->apbs", front_l, panel_e.astype(jnp.float32), precision=highest
        )
        wide_a = mask_a[:, None, :, None]
        wide_b = mask_b[:, None, :, None]
        current_c = current_c - jnp.where(wide_a, term_c, 0.0) + jnp.where(wide_b, gain_c, 0.0)
        current_f = current_f - jnp.where(wide_a, term_f, 0.0) + jnp.where(wide_b, gain_f, 0.0)
        place = (owned[None, :] & (local_rows[:, None] == own_slot[None, :]))[:, None, :, None]
        out_r = out_r + jnp.where(place, new_r.transpose(1, 0, 2)[None], 0.0)
        out_l = out_l + jnp.where(place, new_l.transpose(1, 0, 2)[None], 0.0)
    return (current_c, current_f, out_r, out_l)


def solution(mesh):
    in_specs = (
        P(None, "row", None, "col"),
        P(None, "row", None, "col"),
        P(None, "row", None, "col"),
        P(None, "row", None, "col"),
        P(None, "row", None, "col"),
        P(None, "row", None, "col"),
        P(None, "row", None),
        P(None, "row", None),
        P(None, "row", None),
        P(None, "row"),
        P(None, "col", None),
        P(None, "col", None),
        P(None, "col", None),
        P(None, "col"),
    )
    out_specs = (
        P(None, "row", None, "col"),
        P(None, "row", None, "col"),
        P(None, "row", None, "col"),
        P(None, "row", None, "col"),
    )
    return jax.shard_map(body, mesh=mesh, in_specs=in_specs, out_specs=out_specs, check_vma=False)
```

profile of v0, /device:TPU:0, one launch (start us, length us, event | category | flops | bytes accessed | tf_op | source)
XLA Modules:
  0.0 719.9 jit_solution(12369988336342731525)
XLA Ops:
  7.2 3.1 copy.81
  10.3 4.3 copy.82
  14.6 4.4 pad_maximum_fusion.2
  22.0 3.0 collective-permute-start.1
  32.4 6.0 copy.88
  38.4 3.7 gather_fusion.4
  45.1 6.1 copy.91
  88.0 136.5 %collective-permute-done = bf16[2,12,128,6,128]{2,4,3,1,0:T(8,128)(2,1)} collective-permute-done((bf16[2,12,128,6,128]{2,4,3,1,0:T(8,128)(2,1)}, bf16[2,12,128,6,128]{2,4,3,1,0:T(8,128)(2,1)}, u32[]{:S(2)}, u32[]{:S(2)}) %collective-permute-start) | collective-permute-done | bytes 4718624 | tf_op jit(solution)/shard_map/ppermute | solution.py:18
  226.7 6.9 pad_maximum_fusion
  233.7 6.2 fusion.108
  239.9 6.6 copy.83
  246.5 5.8 gather_fusion.27
  272.5 6.9 pad_maximum_fusion.1
  279.5 6.4 slice_bitcast_fusion
  285.9 6.0 gather_fusion.28
  302.4 6.6 copy.93
  309.0 6.0 gather_fusion.29
  320.4 6.7 copy.106
  327.1 5.9 gather_fusion.30
  333.0 5.2 fusion.14
  338.2 6.0 gather_fusion.32
  348.0 3.1 slice_bitcast_fusion.11
  351.1 3.1 slice_bitcast_fusion.6
  356.4 5.9 gather_fusion.31
  362.4 5.3 fusion.13
  367.7 5.2 fusion.31
  372.9 14.3 %all-reduce.7.cloned.1.call-done = f32[6,128,128]{2,1,0:T(8,128)} async-done(((f32[6,128,128]{2,1,0:T(8,128)}), f32[6,128,128]{2,1,0:T(8,128)}) %all-reduce.7.cloned.1.call-update) | async-done | bytes 393232 | tf_op jit(solution)/shard_map/psum | solution.py:126
  387.3 10.1 %fusion.11 = f32[12,128,6,128]{1,3,0,2:T(8,128)} fusion(f32[12,128,6,128]{1,3,0,2:T(8,128)} %copy.88, f32[12,128,6,128]{1,3,0,2:T(8,128)} %fusion.31, pred[12,6]{0,1:T(8,128)(4,1)S(1)} %copy-done.48, pred[12,6]{0,1:T(8,128)(4,1)S(1)} %copy-done.49, f32[6,128,128]{2,1,0:T(8,128)} %all-reduce.7.cloned.1.call-done, pred[6]{0:T(512)(128)(4,1)S(1)} %copy-done.65, ...), kind=kOutput, calls=%fused_computation.57 | convolution fusion | flops 1816756224 | bytes 16908438 | tf_op jit(solution)/shard_map/apbq,bqs->apbs/dot_general | solution.py:132
  400.4 4.4 fusion.29
  404.9 7.1 fusion.9
  422.6 3.4 slice_bitcast_fusion.7
  426.0 3.1 gather_fusion.16
  442.9 55.0 %all-reduce.13.cloned.1.call-done = f32[12,128,128]{2,1,0:T(8,128)} async-done(((f32[12,128,128]{2,1,0:T(8,128)}), f32[12,128,128]{2,1,0:T(8,128)}) %all-reduce.13.cloned.1.call-update) | async-done | bytes 786448 | tf_op jit(solution)/shard_map/psum | solution.py:128
  497.9 5.4 fusion.27
  503.3 29.3 %all-reduce.11.cloned.1.call-done = f32[6,128,128]{2,1,0:T(8,128)} async-done(((f32[6,128,128]{2,1,0:T(8,128)}), f32[6,128,128]{2,1,0:T(8,128)}) %all-reduce.11.cloned.1.call-update) | async-done | bytes 393232 | tf_op jit(solution)/shard_map/psum | solution.py:126
  532.7 10.2 %fusion.7 = f32[12,128,6,128]{1,3,0,2:T(8,128)} fusion(f32[12,128,6,128]{1,3,0,2:T(8,128)} %fusion.11, f32[12,128,6,128]{1,3,0,2:T(8,128)} %fusion.27, pred[12,6]{0,1:T(8,128)(4,1)S(1)} %copy-done.47, pred[12,6]{0,1:T(8,128)(4,1)S(1)} %copy-done.46, f32[6,128,128]{2,1,0:T(8,128)} %all-reduce.11.cloned.1.call-done, pred[6]{0:T(512)(128)(4,1)} %copy-done.50, ...), kind=kOutput, calls=%fused_computation.51 | convolution fusion | flops 1816756224 | bytes 16908944 | tf_op jit(solution)/shard_map/apbq,bqs->apbs/dot_general | solution.py:132
  545.9 4.4 fusion.25
  550.4 7.2 %fusion.5 = f32[12,128,6,128]{1,3,0,2:T(8,128)} fusion(f32[12,128,6,128]{1,3,0,2:T(8,128)} %fusion.9, f32[12,128,6,128]{1,3,0,2:T(8,128)S(1)} %fusion.25, pred[12,6]{0,1:T(8,128)(4,1)S(1)} %copy-done.47, pred[12,6]{0,1:T(8,128)(4,1)S(1)} %copy-done.46, bf16[2,12,128,6,128]{4,2,1,3,0:T(8,128)(2,1)S(1)} %bitcast.225, f32[6,128,128]{2,1,0:T(8,128)S(1)} %copy-done.40, ...), kind=kOutput, calls=%fused_computation.48 | convolution fusion | flops 1816756224 | bytes 16910848 | tf_op jit(solution)/shard_map/apbq,bqs->apbs/dot_general | solution.py:135
  572.0 6.3 select_add_fusion
  578.3 6.1 copy.127
  584.4 6.2 copy.128
  590.7 53.6 %all-reduce.17.cloned.1.call-done = f32[12,128,128]{2,1,0:T(8,128)} async-done(((f32[12,128,128]{2,1,0:T(8,128)}), f32[12,128,128]{2,1,0:T(8,128)}) %all-reduce.17.cloned.1.call-update) | async-done | bytes 786448 | tf_op jit(solution)/shard_map/psum | solution.py:128
  644.2 5.2 fusion.21
  649.5 28.9 %all-reduce.15.cloned.1.call-done = f32[6,128,128]{2,1,0:T(8,128)} async-done(((f32[6,128,128]{2,1,0:T(8,128)}), f32[6,128,128]{2,1,0:T(8,128)}) %all-reduce.15.cloned.1.call-update) | async-done | bytes 393232 | tf_op jit(solution)/shard_map/psum | solution.py:126
  678.4 10.1 %fusion.1 = f32[12,128,6,128]{1,3,0,2:T(8,128)} fusion(f32[12,128,6,128]{1,3,0,2:T(8,128)} %fusion.5, f32[12,128,6,128]{1,3,0,2:T(8,128)} %fusion.21, pred[12,6]{0,1:T(8,128)(4,1)S(1)} %copy-done.45, pred[12,6]{0,1:T(8,128)(4,1)S(1)} %get-tuple-element.34, bf16[2,12,128,6,128]{4,2,1,3,0:T(8,128)(2,1)} %fusion.13, ...), kind=kOutput, calls=%fused_computation.42 | convolution fusion | flops 1816756224 | bytes 16908438 | tf_op jit(solution)/shard_map/apbq,bqs->apbs/dot_general | solution.py:135
  688.5 6.5 copy.126
  697.7 8.8 %fusion.3 = f32[12,128,6,128]{1,3,0,2:T(8,128)} fusion(f32[12,128,6,128]{1,3,0,2:T(8,128)} %fusion.7, f32[12,128,6,128]{1,3,0,2:T(8,128)S(1)} %fusion.23, pred[12,6]{0,1:T(8,128)(4,1)S(1)} %copy-done.45, pred[12,6]{0,1:T(8,128)(4,1)S(1)} %get-tuple-element.34, f32[6,128,128]{2,1,0:T(8,128)S(1)} %copy-done.41, pred[6]{0:T(512)(128)(4,1)S(1)} %copy-done.61, ...), kind=kOutput, calls=%fused_computation.45 | convolution fusion | flops 1816756224 | bytes 16908438 | tf_op jit(solution)/shard_map/apbq,bqs->apbs/dot_general | solution.py:132
  706.5 6.0 copy.125
  (305 shorter events, 140.9 us)
Async XLA Ops:
  7.2 44.0 %copy-start = (f32[12,128,128]{2,1,0:T(8,128)S(1)}, f32[12,128,128]{2,1,0:T(8,128)}, u32[]{:S(2)}) copy-start(f32[12,128,128]{2,1,0:T(8,128)} %param.24) | copy-start | bytes 2359300
  7.2 360.5 %all-reduce.9.cloned.1.call-start = ((), (), s32[]{:S(2)}) async-start(), calls=%async_computation.1 | async-start | bytes 1572864 | tf_op jit(solution)/shard_map/psum | solution.py:128
  14.6 10.5 %copy-start.7 = (bf16[12,128,6,128]{3,1,2,0:T(8,128)(2,1)S(1)}, bf16[12,128,6,128]{3,1,2,0:T(8,128)(2,1)}, u32[]{:S(2)}) copy-start(bf16[12,128,6,128]{3,1,2,0:T(8,128)(2,1)} %param.23) | copy-start | bytes 7077892
  14.6 10.5 %copy-start.9 = (bf16[12,128,6,128]{3,1,2,0:T(8,128)(2,1)S(1)}, bf16[12,128,6,128]{3,1,2,0:T(8,128)(2,1)}, u32[]{:S(2)}) copy-start(bf16[12,128,6,128]{3,1,2,0:T(8,128)(2,1)} %param.22) | copy-start | bytes 7077892
  19.0 205.5 %collective-permute-start = (bf16[2,12,128,6,128]{2,4,3,1,0:T(8,128)(2,1)}, bf16[2,12,128,6,128]{2,4,3,1,0:T(8,128)(2,1)}, u32[]{:S(2)}, u32[]{:S(2)}) collective-permute-start(bf16[2,12,128,6,128]{2,4,3,1,0:T(8,128)(2,1)} %pad_maximum_fusion.2), channel_id=1, source_target_pairs={{0,1},{1,2},{2,3},{3,4},{4,5},{5,6},{6,7},{7,0},{8,9},{9,10},{10,1... | collective-permute-start | bytes 14155784 | tf_op jit(solution)/shard_map/ppermute | solution.py:18
  22.0 204.7 %collective-permute-start.1 = (bf16[2,12,128,6,128]{2,4,3,1,0:T(8,128)(2,1)}, bf16[2,12,128,6,128]{2,4,3,1,0:T(8,128)(2,1)}, u32[]{:S(2)}, u32[]{:S(2)}) collective-permute-start(bf16[2,12,128,6,128]{2,4,3,1,0:T(8,128)(2,1)} %pad_maximum_fusion.2), channel_id=1, source_target_pairs={{1,0},{2,1},{3,2},{4,3},{5,4},{6,5},{7,6},{0,7},{9,8},{10,9},{11,1... | collective-permute-start | bytes 14155784 | tf_op jit(solution)/shard_map/ppermute | solution.py:19
  27.7 244.8 %collective-permute-start.2 = (bf16[2,12,128,6,128]{4,2,3,1,0:T(8,128)(2,1)}, bf16[2,12,128,6,128]{4,2,3,1,0:T(8,128)(2,1)}, u32[]{:S(2)}, u32[]{:S(2)}) collective-permute-start(bf16[2,12,128,6,128]{4,2,3,1,0:T(8,128)(2,1)} %pad_maximum_fusion.3), channel_id=1, source_target_pairs={{0,8},{8,16},{16,24},{24,0},{1,9},{9,17},{17,25},{25,1},{2,10},{10... | collective-permute-start | bytes 14155784 | tf_op jit(solution)/shard_map/ppermute | solution.py:18
  27.7 244.8 %collective-permute-start.3 = (bf16[2,12,128,6,128]{4,2,3,1,0:T(8,128)(2,1)}, bf16[2,12,128,6,128]{4,2,3,1,0:T(8,128)(2,1)}, u32[]{:S(2)}, u32[]{:S(2)}) collective-permute-start(bf16[2,12,128,6,128]{4,2,3,1,0:T(8,128)(2,1)} %pad_maximum_fusion.3), channel_id=1, source_target_pairs={{8,0},{16,8},{24,16},{0,24},{9,1},{17,9},{25,17},{1,25},{10,2},{18... | collective-permute-start | bytes 14155784 | tf_op jit(solution)/shard_map/ppermute | solution.py:19
  30.0 12.1 %copy-start.43 = (s32[6]{0:T(128)}, s32[6]{0:T(128)S(1)}, u32[]{:S(2)}) copy-start(s32[6]{0:T(128)S(1)} %get-tuple-element.62) | copy-start | bytes 76
  45.1 14.2 %copy-start.42 = (f32[12,128]{1,0:T(8,128)S(1)}, f32[12,128]{1,0:T(8,128)}, u32[]{:S(2)}) copy-start(f32[12,128]{1,0:T(8,128)} %param.27) | copy-start | bytes 18436
  76.0 157.6 %copy-start.66 = (pred[12]{0:T(512)(128)(4,1)}, pred[12]{0:T(512)(128)(4,1)S(1)}, u32[]{:S(2)}) copy-start(pred[12]{0:T(512)(128)(4,1)S(1)} %compare_and_fusion.18) | copy-start | bytes 40
  76.0 157.6 %copy-start.64 = (pred[6]{0:T(512)(128)(4,1)}, pred[6]{0:T(512)(128)(4,1)S(1)}, u32[]{:S(2)}) copy-start(pred[6]{0:T(512)(128)(4,1)S(1)} %compare_and_fusion.20) | copy-start | bytes 22
  78.3 155.3 %copy-start.56 = (pred[6]{0:T(512)(128)(4,1)}, pred[6]{0:T(512)(128)(4,1)S(1)}, u32[]{:S(2)}) copy-start(pred[6]{0:T(512)(128)(4,1)S(1)} %get-tuple-element.55) | copy-start | bytes 22
  78.4 155.3 %copy-start.50 = (pred[6]{0:T(512)(128)(4,1)}, pred[6]{0:T(512)(128)(4,1)S(1)}, u32[]{:S(2)}) copy-start(pred[6]{0:T(512)(128)(4,1)S(1)} %get-tuple-element.57) | copy-start | bytes 22
  78.4 155.3 %copy-start.54 = (pred[6]{0:T(512)(128)(4,1)}, pred[6]{0:T(512)(128)(4,1)S(1)}, u32[]{:S(2)}) copy-start(pred[6]{0:T(512)(128)(4,1)S(1)} %get-tuple-element.56) | copy-start | bytes 22
  78.4 155.3 %copy-start.58 = (pred[12]{0:T(512)(128)(4,1)}, pred[12]{0:T(512)(128)(4,1)S(1)}, u32[]{:S(2)}) copy-start(pred[12]{0:T(512)(128)(4,1)S(1)} %get-tuple-element.44) | copy-start | bytes 40
  78.4 155.3 %copy-start.62 = (pred[12]{0:T(512)(128)(4,1)}, pred[12]{0:T(512)(128)(4,1)S(1)}, u32[]{:S(2)}) copy-start(pred[12]{0:T(512)(128)(4,1)S(1)} %get-tuple-element.45) | copy-start | bytes 40
  79.0 154.7 %copy-start.60 = (pred[6]{0:T(512)(128)(4,1)}, pred[6]{0:T(512)(128)(4,1)S(1)}, u32[]{:S(2)}) copy-start(pred[6]{0:T(512)(128)(4,1)S(1)} %get-tuple-element.53) | copy-start | bytes 22
  79.5 7.9 %copy-start.52 = (pred[6]{0:T(512)(128)(4,1)}, pred[6]{0:T(512)(128)(4,1)S(1)}, u32[]{:S(2)}) copy-start(pred[6]{0:T(512)(128)(4,1)S(1)} %get-tuple-element.51) | copy-start | bytes 22
  258.9 8.6 %copy-start.19 = (f32[6,128,128]{2,1,0:T(8,128)S(1)}, f32[6,128,128]{2,1,0:T(8,128)}, u32[]{:S(2)}) copy-start(f32[6,128,128]{2,1,0:T(8,128)} %param.30) | copy-start | bytes 1179652
  262.7 9.9 %copy-start.8 = (bf16[12,128,6,128]{3,1,2,0:T(8,128)(2,1)S(1)}, bf16[12,128,6,128]{3,1,2,0:T(8,128)(2,1)}, u32[]{:S(2)}) copy-start(bf16[12,128,6,128]{3,1,2,0:T(8,128)(2,1)} %param.23) | copy-start | bytes 7077892
  297.2 11.8 %copy-start.6 = (bf16[12,128,6,128]{3,1,2,0:T(8,128)(2,1)}, bf16[12,128,6,128]{3,1,2,0:T(8,128)(2,1)S(1)}, u32[]{:S(2)}) copy-start(bf16[12,128,6,128]{3,1,2,0:T(8,128)(2,1)S(1)} %get-tuple-element.28) | copy-start | bytes 7077892
  302.4 84.9 %all-reduce.7.cloned.1.call-start = ((), (), s32[]{:S(2)}) async-start(), calls=%async_computation | async-start | bytes 786432 | tf_op jit(solution)/shard_map/psum | solution.py:126
  354.2 143.6 %all-reduce.13.cloned.1.call-start = ((), (), s32[]{:S(2)}) async-start(), calls=%async_computation.3 | async-start | bytes 1572864 | tf_op jit(solution)/shard_map/psum | solution.py:128
  367.6 19.6 %copy-start.48 = (pred[12,6]{0,1:T(8,128)(4,1)S(1)}, pred[12,6]{0,1:T(8,128)(4,1)}, u32[]{:S(2)}) copy-start(pred[12,6]{0,1:T(8,128)(4,1)} %get-tuple-element.36) | copy-start | bytes 220
  367.6 19.6 %copy-start.49 = (pred[12,6]{0,1:T(8,128)(4,1)S(1)}, pred[12,6]{0,1:T(8,128)(4,1)}, u32[]{:S(2)}) copy-start(pred[12,6]{0,1:T(8,128)(4,1)} %get-tuple-element.37) | copy-start | bytes 220
  367.6 19.6 %copy-start.65 = (pred[6]{0:T(512)(128)(4,1)S(1)}, pred[6]{0:T(512)(128)(4,1)}, u32[]{:S(2)}) copy-start(pred[6]{0:T(512)(128)(4,1)} %copy-done.64) | copy-start | bytes 22
  387.3 13.2 %copy-start.25 = (f32[12,128,128]{2,1,0:T(8,128)S(1)}, f32[12,128,128]{2,1,0:T(8,128)}, u32[]{:S(2)}) copy-start(f32[12,128,128]{2,1,0:T(8,128)} %all-reduce.9.cloned.1.call-done) | copy-start | bytes 2359300
  404.9 10.2 %copy-start.38 = (f32[6,128,128]{2,1,0:T(8,128)S(1)}, f32[6,128,128]{2,1,0:T(8,128)}, u32[]{:S(2)}) copy-start(f32[6,128,128]{2,1,0:T(8,128)} %fusion.113) | copy-start | bytes 1179652
  404.9 11.2 %copy-start.17 = (f32[6,128,128]{2,1,0:T(8,128)S(1)}, f32[6,128,128]{2,1,0:T(8,128)}, u32[]{:S(2)}) copy-start(f32[6,128,128]{2,1,0:T(8,128)} %param.28) | copy-start | bytes 1179652
  404.9 12.0 %copy-start.35 = (f32[6,128,128]{2,1,0:T(8,128)S(1)}, f32[6,128,128]{2,1,0:T(8,128)}, u32[]{:S(2)}) copy-start(f32[6,128,128]{2,1,0:T(8,128)} %gather_fusion.12) | copy-start | bytes 1179652
  426.0 71.9 %copy-start.11 = (bf16[12,128,6,128]{3,1,2,0:T(8,128)(2,1)S(1)}, bf16[12,128,6,128]{3,1,2,0:T(8,128)(2,1)}, u32[]{:S(2)}) copy-start(bf16[12,128,6,128]{3,1,2,0:T(8,128)(2,1)} %get-tuple-element.27) | copy-start | bytes 7077892
  441.8 90.8 %copy-start.46 = (pred[12,6]{0,1:T(8,128)(4,1)S(1)}, pred[12,6]{0,1:T(8,128)(4,1)}, u32[]{:S(2)}) copy-start(pred[12,6]{0,1:T(8,128)(4,1)} %get-tuple-element.32) | copy-start | bytes 220
  441.8 90.8 %copy-start.47 = (pred[12,6]{0,1:T(8,128)(4,1)S(1)}, pred[12,6]{0,1:T(8,128)(4,1)}, u32[]{:S(2)}) copy-start(pred[12,6]{0,1:T(8,128)(4,1)} %get-tuple-element.33) | copy-start | bytes 220
  441.8 90.8 %all-reduce.11.cloned.1.call-start = ((), (), s32[]{:S(2)}) async-start(), calls=%async_computation.2 | async-start | bytes 786432 | tf_op jit(solution)/shard_map/psum | solution.py:126
  442.9 201.3 %all-reduce.17.cloned.1.call-start = ((), (), s32[]{:S(2)}) async-start(), calls=%async_computation.5 | async-start | bytes 1572864 | tf_op jit(solution)/shard_map/psum | solution.py:128
  532.7 13.2 %copy-start.27 = (f32[12,128,128]{2,1,0:T(8,128)S(1)}, f32[12,128,128]{2,1,0:T(8,128)}, u32[]{:S(2)}) copy-start(f32[12,128,128]{2,1,0:T(8,128)} %all-reduce.13.cloned.1.call-done) | copy-start | bytes 2359300
  532.7 13.2 %copy-start.63 = (pred[12]{0:T(512)(128)(4,1)S(1)}, pred[12]{0:T(512)(128)(4,1)}, u32[]{:S(2)}) copy-start(pred[12]{0:T(512)(128)(4,1)} %copy-done.62) | copy-start | bytes 40
  550.4 10.3 %copy-start.36 = (f32[6,128,128]{2,1,0:T(8,128)S(1)}, f32[6,128,128]{2,1,0:T(8,128)}, u32[]{:S(2)}) copy-start(f32[6,128,128]{2,1,0:T(8,128)} %fusion.117) | copy-start | bytes 1179652
  550.4 11.2 %copy-start.18 = (f32[6,128,128]{2,1,0:T(8,128)S(1)}, f32[6,128,128]{2,1,0:T(8,128)}, u32[]{:S(2)}) copy-start(f32[6,128,128]{2,1,0:T(8,128)} %param.28) | copy-start | bytes 1179652
  550.4 12.1 %copy-start.33 = (f32[6,128,128]{2,1,0:T(8,128)S(1)}, f32[6,128,128]{2,1,0:T(8,128)}, u32[]{:S(2)}) copy-start(f32[6,128,128]{2,1,0:T(8,128)} %gather_fusion.21) | copy-start | bytes 1179652
  563.0 7.6 %copy-start.22 = (f32[6,128,128]{2,1,0:T(8,128)S(1)}, f32[6,128,128]{2,1,0:T(8,128)}, u32[]{:S(2)}) copy-start(f32[6,128,128]{2,1,0:T(8,128)} %gather_fusion.18) | copy-start | bytes 1179652
  571.7 106.7 %all-reduce.15.cloned.1.call-start = ((), (), s32[]{:S(2)}) async-start(), calls=%async_computation.4 | async-start | bytes 786432 | tf_op jit(solution)/shard_map/psum | solution.py:126
  584.4 59.8 %copy-start.5 = (bf16[12,128,6,128]{3,1,2,0:T(8,128)(2,1)S(1)}, bf16[12,128,6,128]{3,1,2,0:T(8,128)(2,1)}, u32[]{:S(2)}) copy-start(bf16[12,128,6,128]{3,1,2,0:T(8,128)(2,1)} %get-tuple-element.24) | copy-start | bytes 7077892
  584.4 59.8 %copy-start.59 = (pred[12]{0:T(512)(128)(4,1)S(1)}, pred[12]{0:T(512)(128)(4,1)}, u32[]{:S(2)}) copy-start(pred[12]{0:T(512)(128)(4,1)} %copy-done.58) | copy-start | bytes 40
  590.6 87.8 %copy-start.45 = (pred[12,6]{0,1:T(8,128)(4,1)S(1)}, pred[12,6]{0,1:T(8,128)(4,1)}, u32[]{:S(2)}) copy-start(pred[12,6]{0,1:T(8,128)(4,1)} %get-tuple-element.35) | copy-start | bytes 220
  590.6 87.8 %copy-start.61 = (pred[6]{0:T(512)(128)(4,1)S(1)}, pred[6]{0:T(512)(128)(4,1)}, u32[]{:S(2)}) copy-start(pred[6]{0:T(512)(128)(4,1)} %copy-done.60) | copy-start | bytes 22
  697.7 14.8 %copy-start.1 = (f32[12,128,128]{2,1,0:T(8,128)S(1)}, f32[12,128,128]{2,1,0:T(8,128)}, u32[]{:S(2)}) copy-start(f32[12,128,128]{2,1,0:T(8,128)} %param.24) | copy-start | bytes 2359300
  (46 other events, 259.6 us)
Sparse Core Ops, SparseCore 0:
  272.6 75.0 all-reduce.8
  354.4 32.8 all-reduce.6
  422.7 75.0 all-reduce.12
  500.7 31.9 all-reduce.10
  569.1 75.0 all-reduce.16
  646.4 31.9 all-reduce.14
where the time goes:
time: 731 us; the launch traced here: 720 us
  waiting for transfers between devices  320 us (44%)
  local copies, waits for them, and re-layouts  194 us (27%)
  matrix products  112 us (15%)
  other arithmetic  70 us (10%)
  between operations  16 us (2%)
  starting transfers between devices  8.39 us (1%)
    ppermute x2, waiting for transfers between devices, padded(): before = lax.ppermute(last, axis, up)  137 us
    psum x3, waiting for transfers between devices, body(): front_l = lax.psum(picked, 'col')  109 us
    psum x3, waiting for transfers between devices, body(): front_r = lax.psum(new_r, 'row')  72.6 us
    unnamed x176, local copies, waits for them, and re-layouts  49.8 us
    dot_general x27, matrix products, product(): jnp.einsum('bij,bjk->bik', left, right, precision=lax.Precision.HIGHEST)  30.8 us
    dot_general x3, matrix products, body(): jnp.einsum('apbq,bqs->apbs', panel_a.astype(jnp.float32), front_r, precis...  29.1 us
    slice x4, local copies, waits for them, and re-layouts, body(): picked_ad = jnp.take(near_ad[:, :, :, :, 1 + offset, :], slot_cols, axis=3)  26.2 us
    dot_general x3, matrix products, body(): jnp.einsum('apbq,bqs->apbs', panel_d.astype(jnp.float32), front_r, precis...  24.4 us
  transfers between devices with their start and end apart: 10, of which 7 were waited for; matrix products, arithmetic and copies ran while one was open for 35% of the time, Pallas kernels for 0%

commit v1 on v0

--- a/solution.py
+++ b/solution.py
@@ -6,6 +6,11 @@
 TILE = 128
 ORDER = 6144
 STEPS = 3
+
+
+def summed_here(x, axis):
+    terms = lax.all_gather(x, axis)
+    return jnp.sum(terms, axis=0)
 
 
 def padded(value, sides, width):
@@ -125,7 +130,7 @@
         l_slot = jnp.clip(cols_clip // count_cols, 0, cols_dev - 1)
         front_r = lax.psum(new_r, "row")
         picked = jnp.where((cols_clip % count_cols == this_col)[:, None, None], new_l[l_slot], 0.0)
-        front_l = lax.psum(picked, "col")
+        front_l = summed_here(picked, "col")
         front_r = jnp.where(col_valid[:, None, None], front_r, 0.0)
         front_l = jnp.where(row_valid[:, None, None], front_l, 0.0)
         mask_a = (block_rows[:, None] < front_rows[None, :]) & col_valid[None, :]

time: 731 us -> 800 us (1.094)
  waiting for transfers between devices: 320 us -> 380 us
    ppermute x2, waiting for transfers between devices: 137 us -> 256 us  [padded(): before = lax.ppermute(last, axis, up)]
    psum x3 -> x0, waiting for transfers between devices: 109 us -> none  [body(): front_l = lax.psum(picked, 'col')]
    all_gather x0 -> x3, waiting for transfers between devices: none -> 106 us  [summed_here(): terms = lax.all_gather(x, axis)]
    psum x3, waiting for transfers between devices: 72.6 us -> 14.1 us  [body(): front_r = lax.psum(new_r, 'row')]
    reduce_sum x0 -> x3, other arithmetic: none -> 10.9 us  [summed_here(): return jnp.sum(terms, axis=0)]
    unnamed x176 -> x144, local copies, waits for them, and re-layouts: 49.8 us -> 51 us
  transfers between devices with their start and end apart: 10 -> 10, of which waited for: 7 -> 7; matrix products, arithmetic and copies ran while one was open for 35% -> 28% of each run, Pallas kernels for 0% -> 0%
where the time goes in v1:
time: 800 us; the launch traced here: 790 us
  waiting for transfers between devices  380 us (48%)
  local copies, waits for them, and re-layouts  192 us (24%)
  matrix products  118 us (15%)
  other arithmetic  75.2 us (9%)
  between operations  16.7 us (2%)
  starting transfers between devices  8.39 us (1%)
    ppermute x2, waiting for transfers between devices, padded(): before = lax.ppermute(last, axis, up)  256 us
    all_gather x3, waiting for transfers between devices, summed_here(): terms = lax.all_gather(x, axis)  106 us
    unnamed x144, local copies, waits for them, and re-layouts  51 us
    dot_general x27, matrix products, product(): jnp.einsum('bij,bjk->bik', left, right, precision=lax.Precision.HIGHEST)  34.5 us
    dot_general x3, matrix products, body(): jnp.einsum('apbq,bqs->apbs', panel_d.astype(jnp.float32), front_r, precis...  30.2 us
    dot_general x3, matrix products, body(): jnp.einsum('apbq,bqs->apbs', panel_a.astype(jnp.float32), front_r, precis...  29 us
    slice x4, local copies, waits for them, and re-layouts, body(): picked_ad = jnp.take(near_ad[:, :, :, :, 1 + offset, :], slot_cols, axis=3)  26.1 us
    gather x3, local copies, waits for them, and re-layouts, body(): picked_be = jnp.take(near_be[:, :, 1 - offset, :, :, :], slot_rows, axis=1)  18 us
  transfers between devices with their start and end apart: 10, of which 7 were waited for; matrix products, arithmetic and copies ran while one was open for 28% of the time, Pallas kernels for 0%

profile of v1, /device:TPU:0, one launch (start us, length us, event | category | flops | bytes accessed | tf_op | source)
XLA Modules:
  0.0 790.5 jit_solution(7011367712666069996)
XLA Ops:
  8.1 3.1 copy.129
  11.2 4.3 copy.130
  15.4 4.3 pad_maximum_fusion.2
  19.7 3.0 collective-permute-start
  22.7 3.0 collective-permute-start.1
  29.2 3.8 gather_fusion.4
  43.5 181.8 %collective-permute-done = bf16[2,12,128,6,128]{2,4,3,1,0:T(8,128)(2,1)} collective-permute-done((bf16[2,12,128,6,128]{2,4,3,1,0:T(8,128)(2,1)}, bf16[2,12,128,6,128]{2,4,3,1,0:T(8,128)(2,1)}, u32[]{:S(2)}, u32[]{:S(2)}) %collective-permute-start) | collective-permute-done | bytes 4718624 | tf_op jit(solution)/shard_map/ppermute | solution.py:23
  227.4 6.9 pad_maximum_fusion
  234.3 6.2 fusion.108
  240.5 6.6 copy.131
  247.1 5.9 gather_fusion.27
  273.2 4.3 pad_maximum_fusion.3
  279.7 6.3 copy.136
  286.0 6.1 copy.139
  305.5 74.1 %collective-permute-done.2 = bf16[2,12,128,6,128]{4,2,3,1,0:T(8,128)(2,1)} collective-permute-done((bf16[2,12,128,6,128]{4,2,3,1,0:T(8,128)(2,1)}, bf16[2,12,128,6,128]{4,2,3,1,0:T(8,128)(2,1)}, u32[]{:S(2)}, u32[]{:S(2)}) %collective-permute-start.2) | collective-permute-done | bytes 4718624 | tf_op jit(solution)/shard_map/ppermute | solution.py:23
  380.9 6.9 pad_maximum_fusion.1
  387.8 6.2 slice_bitcast_fusion
  394.0 6.0 gather_fusion.28
  412.3 6.6 copy.141
  418.9 5.9 gather_fusion.29
  436.7 4.2 reduce_sum.27
  441.0 5.4 fusion.29
  446.4 4.1 fusion.31
  450.5 14.1 %all-reduce.4.cloned.1.call-done = f32[6,128,128]{2,1,0:T(8,128)} async-done(((f32[6,128,128]{2,1,0:T(8,128)}), f32[6,128,128]{2,1,0:T(8,128)}) %all-reduce.4.cloned.1.call-update) | async-done | bytes 393232 | tf_op jit(solution)/shard_map/psum | solution.py:131
  464.6 10.1 %fusion.11 = f32[12,128,6,128]{1,3,0,2:T(8,128)} fusion(f32[12,128,6,128]{1,3,0,2:T(8,128)} %copy.136, f32[12,128,6,128]{1,3,0,2:T(8,128)} %fusion.31, pred[12,6]{0,1:T(8,128)(4,1)S(1)} %copy-done.41, pred[12,6]{0,1:T(8,128)(4,1)S(1)} %copy-done.42, f32[6,128,128]{2,1,0:T(8,128)} %all-reduce.4.cloned.1.call-done, pred[6]{0:T(512)(128)(4,1)S(1)} %copy-done.59, ...), kind=kOutput, calls=%fused_computation.57 | convolution fusion | flops 1816756224 | bytes 16908438 | tf_op jit(solution)/shard_map/apbq,bqs->apbs/dot_general | solution.py:137
  477.7 10.0 %fusion.9 = f32[12,128,6,128]{1,3,0,2:T(8,128)} fusion(f32[12,128,6,128]{1,3,0,2:T(8,128)} %copy.139, f32[12,128,6,128]{1,3,0,2:T(8,128)} %fusion.29, pred[12,6]{0,1:T(8,128)(4,1)S(1)} %copy-done.41, pred[12,6]{0,1:T(8,128)(4,1)S(1)} %copy-done.42, bf16[2,12,128,6,128]{4,2,1,3,0:T(8,128)(2,1)} %copy-done.3, f32[6,128,128]{2,1,0:T(8,128)S(1)} %copy-done.33, ...), kind=kOutput, calls=%fused_computation.54 | convolution fusion | flops 1816756224 | bytes 16908438 | tf_op jit(solution)/shard_map/apbq,bqs->apbs/dot_general | solution.py:140
  508.3 6.1 gather_fusion.30
  514.5 3.1 fusion.14
  521.2 6.6 copy.154
  527.8 5.9 gather_fusion.31
  549.6 49.4 %all-gather.6.cloned.1.call-done = f32[8,12,128,128]{3,2,1,0:T(8,128)} async-done(((f32[1,12,128,128]{3,2,1,0:T(8,128)}), f32[8,12,128,128]{3,2,1,0:T(8,128)}) %all-gather.6.cloned.1.call-update) | async-done | bytes 6291472 | tf_op jit(solution)/shard_map/all_gather | solution.py:12
  599.0 3.3 reduce_sum.28
  602.4 4.0 fusion.25
  606.4 4.4 fusion.27
  610.9 10.1 %fusion.7 = f32[12,128,6,128]{1,3,0,2:T(8,128)} fusion(f32[12,128,6,128]{1,3,0,2:T(8,128)} %fusion.11, f32[12,128,6,128]{1,3,0,2:T(8,128)} %fusion.27, pred[12,6]{0,1:T(8,128)(4,1)S(1)} %copy-done.40, pred[12,6]{0,1:T(8,128)(4,1)S(1)} %copy-done.39, f32[6,128,128]{2,1,0:T(8,128)} %all-reduce.6.cloned.1.call-done, pred[6]{0:T(512)(128)(4,1)S(1)} %copy-done.44, ...), kind=kOutput, calls=%fused_computation.51 | convolution fusion | flops 1816756224 | bytes 16908438 | tf_op jit(solution)/shard_map/apbq,bqs->apbs/dot_general | solution.py:137
  624.0 10.1 %fusion.5 = f32[12,128,6,128]{1,3,0,2:T(8,128)} fusion(f32[12,128,6,128]{1,3,0,2:T(8,128)} %fusion.9, f32[12,128,6,128]{1,3,0,2:T(8,128)} %fusion.25, pred[12,6]{0,1:T(8,128)(4,1)S(1)} %copy-done.40, pred[12,6]{0,1:T(8,128)(4,1)S(1)} %copy-done.39, bf16[2,12,128,6,128]{4,2,1,3,0:T(8,128)(2,1)} %copy-done.4, f32[6,128,128]{2,1,0:T(8,128)S(1)} %copy-done.35, ...), kind=kOutput, calls=%fused_computation.48 | convolution fusion | flops 1816756224 | bytes 16908438 | tf_op jit(solution)/shard_map/apbq,bqs->apbs/dot_general | solution.py:140
  646.6 5.8 gather_fusion.32
  652.5 3.0 fusion.12
  665.9 6.7 select_add_fusion
  672.6 6.1 copy.175
  678.7 6.0 copy.176
  684.8 56.8 %all-gather.8.cloned.1.call-done = f32[8,12,128,128]{3,2,1,0:T(8,128)} async-done(((f32[1,12,128,128]{3,2,1,0:T(8,128)}), f32[8,12,128,128]{3,2,1,0:T(8,128)}) %all-gather.8.cloned.1.call-update) | async-done | bytes 6291472 | tf_op jit(solution)/shard_map/all_gather | solution.py:12
  741.6 3.3 reduce_sum.29
  745.0 4.0 fusion.21
  749.0 10.1 %fusion.1 = f32[12,128,6,128]{1,3,0,2:T(8,128)} fusion(f32[12,128,6,128]{1,3,0,2:T(8,128)} %fusion.5, f32[12,128,6,128]{1,3,0,2:T(8,128)} %fusion.21, pred[12,6]{0,1:T(8,128)(4,1)S(1)} %copy-done.38, pred[12,6]{0,1:T(8,128)(4,1)S(1)} %copy-done.37, bf16[2,12,128,6,128]{4,2,1,3,0:T(8,128)(2,1)} %copy-done.2, ...), kind=kOutput, calls=%fused_computation.42 | convolution fusion | flops 1816756224 | bytes 16908438 | tf_op jit(solution)/shard_map/apbq,bqs->apbs/dot_general | solution.py:140
  759.0 6.4 copy.174
  768.1 8.7 %fusion.3 = f32[12,128,6,128]{1,3,0,2:T(8,128)} fusion(f32[12,128,6,128]{1,3,0,2:T(8,128)} %fusion.7, f32[12,128,6,128]{1,3,0,2:T(8,128)S(1)} %fusion.23, pred[12,6]{0,1:T(8,128)(4,1)S(1)} %copy-done.38, pred[12,6]{0,1:T(8,128)(4,1)S(1)} %copy-done.37, f32[6,128,128]{2,1,0:T(8,128)S(1)} %copy-done.34, pred[6]{0:T(512)(128)(4,1)S(1)} %copy-done.54, ...), kind=kOutput, calls=%fused_computation.45 | convolution fusion | flops 1816756224 | bytes 16908438 | tf_op jit(solution)/shard_map/apbq,bqs->apbs/dot_general | solution.py:137
  776.9 6.0 copy.173
  (274 shorter events, 148.2 us)
Async XLA Ops:
  8.0 25.7 %copy-start = (f32[12,128,128]{2,1,0:T(8,128)S(1)}, f32[12,128,128]{2,1,0:T(8,128)}, u32[]{:S(2)}) copy-start(f32[12,128,128]{2,1,0:T(8,128)} %param.24) | copy-start | bytes 2359300
  8.0 428.7 %all-gather.4.cloned.1.call-start = ((), (), s32[]{:S(2)}) async-start(), calls=%async_computation.1 | async-start | bytes 7077888 | tf_op jit(solution)/shard_map/all_gather | solution.py:12
  15.4 22.0 %copy-start.36 = (f32[12,128]{1,0:T(8,128)S(1)}, f32[12,128]{1,0:T(8,128)}, u32[]{:S(2)}) copy-start(f32[12,128]{1,0:T(8,128)} %param.27) | copy-start | bytes 18436
  19.7 205.5 %collective-permute-start = (bf16[2,12,128,6,128]{2,4,3,1,0:T(8,128)(2,1)}, bf16[2,12,128,6,128]{2,4,3,1,0:T(8,128)(2,1)}, u32[]{:S(2)}, u32[]{:S(2)}) collective-permute-start(bf16[2,12,128,6,128]{2,4,3,1,0:T(8,128)(2,1)} %pad_maximum_fusion.2), channel_id=1, source_target_pairs={{0,1},{1,2},{2,3},{3,4},{4,5},{5,6},{6,7},{7,0},{8,9},{9,10},{10,1... | collective-permute-start | bytes 14155784 | tf_op jit(solution)/shard_map/ppermute | solution.py:23
  22.7 204.7 %collective-permute-start.1 = (bf16[2,12,128,6,128]{2,4,3,1,0:T(8,128)(2,1)}, bf16[2,12,128,6,128]{2,4,3,1,0:T(8,128)(2,1)}, u32[]{:S(2)}, u32[]{:S(2)}) collective-permute-start(bf16[2,12,128,6,128]{2,4,3,1,0:T(8,128)(2,1)} %pad_maximum_fusion.2), channel_id=1, source_target_pairs={{1,0},{2,1},{3,2},{4,3},{5,4},{6,5},{7,6},{0,7},{9,8},{10,9},{11,1... | collective-permute-start | bytes 14155784 | tf_op jit(solution)/shard_map/ppermute | solution.py:24
  29.2 233.0 %copy-start.14 = (f32[6,128,128]{2,1,0:T(8,128)}, f32[6,128,128]{2,1,0:T(8,128)S(1)}, u32[]{:S(2)}) copy-start(f32[6,128,128]{2,1,0:T(8,128)S(1)} %gather_fusion.1) | copy-start | bytes 1179652
  42.3 225.9 %copy-start.45 = (pred[6]{0:T(512)(128)(4,1)}, pred[6]{0:T(512)(128)(4,1)S(1)}, u32[]{:S(2)}) copy-start(pred[6]{0:T(512)(128)(4,1)S(1)} %get-tuple-element.59) | copy-start | bytes 22
  263.4 9.9 %copy-start.5 = (bf16[12,128,6,128]{3,1,2,0:T(8,128)(2,1)S(1)}, bf16[12,128,6,128]{3,1,2,0:T(8,128)(2,1)}, u32[]{:S(2)}) copy-start(bf16[12,128,6,128]{3,1,2,0:T(8,128)(2,1)} %param.23) | copy-start | bytes 7077892
  277.5 102.2 %collective-permute-start.2 = (bf16[2,12,128,6,128]{4,2,3,1,0:T(8,128)(2,1)}, bf16[2,12,128,6,128]{4,2,3,1,0:T(8,128)(2,1)}, u32[]{:S(2)}, u32[]{:S(2)}) collective-permute-start(bf16[2,12,128,6,128]{4,2,3,1,0:T(8,128)(2,1)} %pad_maximum_fusion.3), channel_id=1, source_target_pairs={{0,8},{8,16},{16,24},{24,0},{1,9},{9,17},{17,25},{25,1},{2,10},{10... | collective-permute-start | bytes 14155784 | tf_op jit(solution)/shard_map/ppermute | solution.py:23
  277.5 103.4 %collective-permute-start.3 = (bf16[2,12,128,6,128]{4,2,3,1,0:T(8,128)(2,1)}, bf16[2,12,128,6,128]{4,2,3,1,0:T(8,128)(2,1)}, u32[]{:S(2)}, u32[]{:S(2)}) collective-permute-start(bf16[2,12,128,6,128]{4,2,3,1,0:T(8,128)(2,1)} %pad_maximum_fusion.3), channel_id=1, source_target_pairs={{8,0},{16,8},{24,16},{0,24},{9,1},{17,9},{25,17},{1,25},{10,2},{18... | collective-permute-start | bytes 14155784 | tf_op jit(solution)/shard_map/ppermute | solution.py:24
  301.2 78.5 %copy-start.60 = (pred[12]{0:T(512)(128)(4,1)}, pred[12]{0:T(512)(128)(4,1)S(1)}, u32[]{:S(2)}) copy-start(pred[12]{0:T(512)(128)(4,1)S(1)} %compare_and_fusion.18) | copy-start | bytes 40
  301.2 78.5 %copy-start.58 = (pred[6]{0:T(512)(128)(4,1)}, pred[6]{0:T(512)(128)(4,1)S(1)}, u32[]{:S(2)}) copy-start(pred[6]{0:T(512)(128)(4,1)S(1)} %compare_and_fusion.20) | copy-start | bytes 22
  302.4 77.3 %copy-start.43 = (pred[6]{0:T(512)(128)(4,1)}, pred[6]{0:T(512)(128)(4,1)S(1)}, u32[]{:S(2)}) copy-start(pred[6]{0:T(512)(128)(4,1)S(1)} %get-tuple-element.61) | copy-start | bytes 22
  302.5 77.2 %copy-start.51 = (pred[12]{0:T(512)(128)(4,1)}, pred[12]{0:T(512)(128)(4,1)S(1)}, u32[]{:S(2)}) copy-start(pred[12]{0:T(512)(128)(4,1)S(1)} %get-tuple-element.48) | copy-start | bytes 40
  302.5 77.2 %copy-start.55 = (pred[12]{0:T(512)(128)(4,1)}, pred[12]{0:T(512)(128)(4,1)S(1)}, u32[]{:S(2)}) copy-start(pred[12]{0:T(512)(128)(4,1)S(1)} %get-tuple-element.49) | copy-start | bytes 40
  303.0 76.7 %copy-start.53 = (pred[6]{0:T(512)(128)(4,1)}, pred[6]{0:T(512)(128)(4,1)S(1)}, u32[]{:S(2)}) copy-start(pred[6]{0:T(512)(128)(4,1)S(1)} %get-tuple-element.57) | copy-start | bytes 22
  412.3 52.3 %all-reduce.4.cloned.1.call-start = ((), (), s32[]{:S(2)}) async-start(), calls=%async_computation | async-start | bytes 786432 | tf_op jit(solution)/shard_map/psum | solution.py:131
  431.4 9.5 %copy-start.61 = (pred[12]{0:T(512)(128)(4,1)S(1)}, pred[12]{0:T(512)(128)(4,1)}, u32[]{:S(2)}) copy-start(pred[12]{0:T(512)(128)(4,1)} %copy-done.60) | copy-start | bytes 40
  431.5 167.6 %all-gather.6.cloned.1.call-start = ((), (), s32[]{:S(2)}) async-start(), calls=%async_computation.3 | async-start | bytes 7077888 | tf_op jit(solution)/shard_map/all_gather | solution.py:12
  446.3 18.3 %copy-start.41 = (pred[12,6]{0,1:T(8,128)(4,1)S(1)}, pred[12,6]{0,1:T(8,128)(4,1)}, u32[]{:S(2)}) copy-start(pred[12,6]{0,1:T(8,128)(4,1)} %get-tuple-element.40) | copy-start | bytes 220
  446.3 18.3 %copy-start.42 = (pred[12,6]{0,1:T(8,128)(4,1)S(1)}, pred[12,6]{0,1:T(8,128)(4,1)}, u32[]{:S(2)}) copy-start(pred[12,6]{0,1:T(8,128)(4,1)} %get-tuple-element.41) | copy-start | bytes 220
  446.3 18.3 %copy-start.59 = (pred[6]{0:T(512)(128)(4,1)S(1)}, pred[6]{0:T(512)(128)(4,1)}, u32[]{:S(2)}) copy-start(pred[6]{0:T(512)(128)(4,1)} %copy-done.58) | copy-start | bytes 22
  464.6 13.0 %copy-start.33 = (f32[6,128,128]{2,1,0:T(8,128)S(1)}, f32[6,128,128]{2,1,0:T(8,128)}, u32[]{:S(2)}) copy-start(f32[6,128,128]{2,1,0:T(8,128)} %all-reduce.4.cloned.1.call-done) | copy-start | bytes 1179652
  477.7 15.2 %copy-start.19 = (f32[6,128,128]{2,1,0:T(8,128)S(1)}, f32[6,128,128]{2,1,0:T(8,128)}, u32[]{:S(2)}) copy-start(f32[6,128,128]{2,1,0:T(8,128)} %param.28) | copy-start | bytes 1179652
  477.7 16.0 %copy-start.29 = (f32[6,128,128]{2,1,0:T(8,128)S(1)}, f32[6,128,128]{2,1,0:T(8,128)}, u32[]{:S(2)}) copy-start(f32[6,128,128]{2,1,0:T(8,128)} %gather_fusion.12) | copy-start | bytes 1179652
  487.8 8.1 %copy-start.28 = (f32[6,128,128]{2,1,0:T(8,128)S(1)}, f32[6,128,128]{2,1,0:T(8,128)}, u32[]{:S(2)}) copy-start(f32[6,128,128]{2,1,0:T(8,128)} %gather_fusion.11) | copy-start | bytes 1179652
  487.8 8.7 %copy-start.22 = (f32[6,128,128]{2,1,0:T(8,128)S(1)}, f32[6,128,128]{2,1,0:T(8,128)}, u32[]{:S(2)}) copy-start(f32[6,128,128]{2,1,0:T(8,128)} %param.30) | copy-start | bytes 1179652
  487.8 8.7 %copy-start.47 = (pred[6]{0:T(512)(128)(4,1)S(1)}, pred[6]{0:T(512)(128)(4,1)}, u32[]{:S(2)}) copy-start(pred[6]{0:T(512)(128)(4,1)} %get-tuple-element.60) | copy-start | bytes 22
  494.2 7.4 copy-start.26
  497.7 16.7 %copy-start.10 = (f32[6,128,128]{2,1,0:T(8,128)}, f32[6,128,128]{2,1,0:T(8,128)S(1)}, u32[]{:S(2)}) copy-start(f32[6,128,128]{2,1,0:T(8,128)S(1)} %get-tuple-element.44) | copy-start | bytes 1179652
  538.7 8.4 %copy-start.24 = (f32[6,128,128]{2,1,0:T(8,128)S(1)}, f32[6,128,128]{2,1,0:T(8,128)}, u32[]{:S(2)}) copy-start(f32[6,128,128]{2,1,0:T(8,128)} %gather_fusion.9) | copy-start | bytes 1179652
  538.7 8.4 %copy-start.48 = (pred[6]{0:T(512)(128)(4,1)S(1)}, pred[6]{0:T(512)(128)(4,1)}, u32[]{:S(2)}) copy-start(pred[6]{0:T(512)(128)(4,1)} %get-tuple-element.60) | copy-start | bytes 22
  547.1 55.3 %copy-start.56 = (pred[12]{0:T(512)(128)(4,1)S(1)}, pred[12]{0:T(512)(128)(4,1)}, u32[]{:S(2)}) copy-start(pred[12]{0:T(512)(128)(4,1)} %copy-done.55) | copy-start | bytes 40
  549.0 61.9 %all-reduce.6.cloned.1.call-start = ((), (), s32[]{:S(2)}) async-start(), calls=%async_computation.2 | async-start | bytes 786432 | tf_op jit(solution)/shard_map/psum | solution.py:131
  549.5 192.0 %all-gather.8.cloned.1.call-start = ((), (), s32[]{:S(2)}) async-start(), calls=%async_computation.5 | async-start | bytes 7077888 | tf_op jit(solution)/shard_map/all_gather | solution.py:12
  610.9 13.0 %copy-start.35 = (f32[6,128,128]{2,1,0:T(8,128)S(1)}, f32[6,128,128]{2,1,0:T(8,128)}, u32[]{:S(2)}) copy-start(f32[6,128,128]{2,1,0:T(8,128)} %all-reduce.6.cloned.1.call-done) | copy-start | bytes 1179652
  624.0 13.1 %copy-start.32 = (f32[6,128,128]{2,1,0:T(8,128)S(1)}, f32[6,128,128]{2,1,0:T(8,128)}, u32[]{:S(2)}) copy-start(f32[6,128,128]{2,1,0:T(8,128)} %fusion.117) | copy-start | bytes 1179652
  624.0 14.1 %copy-start.20 = (f32[6,128,128]{2,1,0:T(8,128)S(1)}, f32[6,128,128]{2,1,0:T(8,128)}, u32[]{:S(2)}) copy-start(f32[6,128,128]{2,1,0:T(8,128)} %param.28) | copy-start | bytes 1179652
  624.0 14.9 %copy-start.31 = (f32[6,128,128]{2,1,0:T(8,128)S(1)}, f32[6,128,128]{2,1,0:T(8,128)}, u32[]{:S(2)}) copy-start(f32[6,128,128]{2,1,0:T(8,128)} %gather_fusion.21) | copy-start | bytes 1179652
  634.1 6.9 copy-start.30
  634.1 7.4 copy-start.23
  634.1 7.4 copy-start.50
  657.9 8.0 %copy-start.62 = (pred[12,6]{0,1:T(8,128)(4,1)S(1)}, pred[12,6]{0,1:T(8,128)(4,1)}, u32[]{:S(2)}) copy-start(pred[12,6]{0,1:T(8,128)(4,1)} %fusion.81) | copy-start | bytes 220
  657.9 8.0 %copy-start.63 = (pred[12,6]{0,1:T(8,128)(4,1)S(1)}, pred[12,6]{0,1:T(8,128)(4,1)}, u32[]{:S(2)}) copy-start(pred[12,6]{0,1:T(8,128)(4,1)} %fusion.82) | copy-start | bytes 220
  664.7 7.9 copy-start.12
  664.9 84.1 %all-reduce.8.cloned.1.call-start = ((), (), s32[]{:S(2)}) async-start(), calls=%async_computation.4 | async-start | bytes 786432 | tf_op jit(solution)/shard_map/psum | solution.py:131
  684.7 60.2 %copy-start.52 = (pred[12]{0:T(512)(128)(4,1)S(1)}, pred[12]{0:T(512)(128)(4,1)}, u32[]{:S(2)}) copy-start(pred[12]{0:T(512)(128)(4,1)} %copy-done.51) | copy-start | bytes 40
  768.1 14.8 %copy-start.1 = (f32[12,128,128]{2,1,0:T(8,128)S(1)}, f32[12,128,128]{2,1,0:T(8,128)}, u32[]{:S(2)}) copy-start(f32[12,128,128]{2,1,0:T(8,128)} %param.24) | copy-start | bytes 2359300
  (30 other events, 139.0 us)
Sparse Core Ops, SparseCore 0:
  273.3 98.7 all-gather.3
  500.3 98.6 all-gather.5
  644.7 96.8 all-gather.7
Sparse Core Ops, SparseCore 1:
  431.6 33.0 all-reduce.3
  552.4 32.7 all-reduce.5
  684.9 31.1 all-reduce.7
